TPU v7x, 32 devices: a whole 2x2x4 slice. The times are simulated.
32 devices in a mesh: groups: 2 (over x), seq: 16 (over z, y, core).
Axes of the slice: x: 2, y: 2, z: 4, core: 2. Of those that a mesh axis runs over, the one named last changes fastest.
Arguments:
- queries: bfloat16 [2048, 4096], P(('groups', 'seq')), parts along dimension 0, may hold values from -8 to 8
- keys: bfloat16 [2048, 512], P(('groups', 'seq')), parts along dimension 0, may hold values from -8 to 8
- values: bfloat16 [2048, 512], P(('groups', 'seq')), parts along dimension 0, may hold values from -6 to 6
- block_pairs: int32 [32], P('groups'), parts along dimension 0, may hold values from 0 to 15, each once
- decode_slots: int32 [32], P('groups'), parts along dimension 0, may hold values from 0 to 15, each once
Outputs:
- attended: bfloat16 [2048, 4096], P(('groups', 'seq')), parts along dimension 0
- decode_cache: bfloat16 [32, 256, 2, 128], P(('groups', 'seq')), parts along dimension 0
There are 2 independent parts, one for each index of `groups`. A program takes and returns all parts, laid end to end along the dimension named above; each array names one. Nothing has to cross between parts.
Inputs may be any that keep to these rules, and one draw needn't show every extreme that they name: `block_pairs`: each of 0 to 15 once. `decode_slots`: each of 0 to 15 once.
All inputs are finite; a program needn't handle non-finite values.
Results may differ from a plain program's by a relative error of at most 0.012.
The roundings to bfloat16 on the way count: a program that leaves them out, or rounds other values in their place, can miss the bound.
Values may be sent and summed in bfloat16 or wider, within the bound.
No kernel may reach another device: no remote copies, remote signals or barrier semaphores. Data moves between devices by JAX's collectives and lax.ppermute only.
A program may use at most 128 MiB of HBM per device.

v0:
```python
import functools
import math

import jax
import jax.numpy as jnp
from jax import lax
from jax.experimental import pallas as pl
from jax.experimental.pallas import tpu as pltpu
from jax.sharding import PartitionSpec as P


HD = 128
KVH = 4
GQ = 8
QH = 32

ROPE_BASE = 500000.0
NEGATIVE = -1e30
LOG2E = math.log2(math.e)

VMEM_SPEC = pl.BlockSpec(memory_space=pltpu.VMEM)
SMEM_SPEC = pl.BlockSpec(memory_space=pltpu.SMEM)
HBM_SPEC = pl.BlockSpec(memory_space=pltpu.HBM)
F32 = jnp.float32
BF16 = jnp.bfloat16


def params(mib):
    return pltpu.CompilerParams(vmem_limit_bytes=mib << 20)


def rotation_tables(block, devices, tok_dev):
    half_tok = tok_dev // 2
    row = lax.broadcasted_iota(jnp.int32, (tok_dev, HD), 0)
    lane = lax.broadcasted_iota(jnp.int32, (tok_dev, HD), 1)
    early = row < half_tok
    position = jnp.where(
        early, block * half_tok + row, (2 * devices - 1 - block) * half_tok + row - half_tok
    )
    low = lane < HD // 2
    index = jnp.where(low, lane, lane - HD // 2).astype(F32)
    frequency = jnp.exp(index * (-2.0 * math.log(ROPE_BASE) / HD))
    angle = position.astype(F32) * frequency
    sine = jnp.sin(angle)
    return jnp.cos(angle), jnp.where(low, -sine, sine)


def turn(block, cosine, sine):
    wide = block.astype(F32)
    return (wide * cosine + pltpu.roll(wide, HD // 2, 1) * sine).astype(BF16)


def prep_kernel(devices, pairs_hbm, k_hbm, v_hbm, kv_ref, trig_ref, pairs_ref, k_ref, sems):
    tok_dev = k_ref.shape[0]
    width = KVH * HD
    pairs_copy = pltpu.make_async_copy(pairs_hbm, pairs_ref, sems.at[0])
    key_copy = pltpu.make_async_copy(k_hbm, k_ref, sems.at[1])
    value_copy = pltpu.make_async_copy(v_hbm, kv_ref.at[:, width:], sems.at[2])
    pairs_copy.start()
    key_copy.start()
    value_copy.start()
    pairs_copy.wait()
    cosine, sine = rotation_tables(pairs_ref[lax.axis_index("seq")], devices, tok_dev)
    trig_ref[:, :HD] = cosine
    trig_ref[:, HD:] = sine
    key_copy.wait()
    for g in range(KVH):
        cols = slice(g * HD, (g + 1) * HD)
        kv_ref[:, cols] = turn(k_ref[:, cols], cosine, sine)
    value_copy.wait()


def prep(pairs, keys, values):
    devices = lax.axis_size("seq")
    tok_dev = keys.shape[0]
    return pl.pallas_call(
        functools.partial(prep_kernel, devices),
        out_shape=(
            jax.ShapeDtypeStruct((tok_dev, 2 * KVH * HD), BF16),
            jax.ShapeDtypeStruct((tok_dev, 2 * HD), F32),
        ),
        in_specs=[HBM_SPEC] * 3,
        out_specs=(VMEM_SPEC, VMEM_SPEC),
        scratch_shapes=[
            pltpu.SMEM((pairs.shape[0],), jnp.int32),
            pltpu.VMEM(keys.shape, BF16),
            pltpu.SemaphoreType.DMA((3,)),
        ],
        compiler_params=params(8),
        name="prep",
    )(pairs, keys, values)


def chunk_kernel(devices, offsets, counts, first, last, *refs):
    refs = list(refs)
    pairs_ref, slots_ref = refs.pop(0), refs.pop(0)
    block_refs = [refs.pop(0) for _ in counts]
    if first:
        q_ref, trig_ref = refs.pop(0), refs.pop(0)
    else:
        turned_ref = refs.pop(0)
        old_refs = [refs.pop(0) for _ in range(3)]
        old_cache_ref = refs.pop(0)
    if first:
        turned_ref = refs.pop(0)
    if last:
        out_ref = refs.pop(0)
    else:
        new_refs = [refs.pop(0) for _ in range(3)]
    cache_ref = refs.pop(0)

    me = lax.axis_index("seq")
    own = pairs_ref[me]
    tok_dev = block_refs[0].shape[-2]
    half_tok = tok_dev // 2
    stride = devices // KVH
    rows = GQ * half_tok

    where = []
    for ref, count in zip(block_refs, counts):
        where += [ref.at[i] for i in range(count)] if count else [ref]
    pair_of = [pairs_ref[lax.bitwise_xor(me, offset)] for offset in offsets]

    if first:
        cosine, sine = trig_ref[:, :HD], trig_ref[:, HD:]
        for g in range(KVH):
            turned = [
                turn(q_ref[:, head * HD : (head + 1) * HD], cosine, sine)
                for head in range(g * GQ, (g + 1) * GQ)
            ]
            for half in range(2):
                part = [t[half * half_tok : (half + 1) * half_tok] for t in turned]
                turned_ref[half, g] = jnp.concatenate(part, axis=0).T

    def gathered(col, half):
        return jnp.concatenate(
            [w[half * half_tok : (half + 1) * half_tok, pl.ds(col, HD)] for w in where], axis=0
        )

    scale = LOG2E / math.sqrt(HD)
    keys_half = len(where) * half_tok

    row = lax.broadcasted_iota(jnp.int32, (half_tok, HD), 0)
    lane = lax.broadcasted_iota(jnp.int32, (half_tok, HD), 1)

    def key_flags(distance):
        column = jnp.where(distance == 0, row, jnp.where(distance < 0, half_tok, HD))
        return jnp.where(lane == column, 1.0, 0.0).astype(BF16)

    early_flags = jnp.concatenate([key_flags(own - pair) for pair in pair_of], axis=0)
    late_flags = jnp.concatenate([key_flags(pair - own) for pair in pair_of], axis=0)
    blank = jnp.zeros((keys_half, HD), BF16)
    order = lax.broadcasted_iota(jnp.int32, (HD, rows), 0)
    token = lax.broadcasted_iota(jnp.int32, (HD, rows), 1) % half_tok
    barred = jnp.where((order > token) & (order <= half_tok), NEGATIVE, 0.0).astype(BF16)
    ones = jnp.ones((16, 2 * keys_half), BF16)

    def scores_of(g):
        key_early, key_late = gathered(g * HD, 0), gathered(g * HD, 1)
        query_early = jnp.concatenate([turned_ref[0, g], barred], axis=0)
        query_late = jnp.concatenate([turned_ref[1, g], barred], axis=0)
        early = jnp.dot(
            jnp.concatenate([key_early, early_flags], axis=1),
            query_early,
            preferred_element_type=F32,
        )
        late_keys = jnp.concatenate([key_early, key_late], axis=0)
        flags = jnp.concatenate([blank, late_flags], axis=0)
        late = jnp.dot(
            jnp.concatenate([late_keys, flags], axis=1), query_late, preferred_element_type=F32
        )
        return early, late

    def update(half, g, scores, values):
        index = half * KVH + g
        top = jnp.max(scores, axis=0, keepdims=True) * scale
        if not first:
            old_max = old_refs[0][index : index + 1, :]
            top = jnp.maximum(old_max, top)
            factor = jnp.exp2(old_max - top)
        weights = jnp.exp2(scores * scale - top).astype(BF16)
        both = jnp.dot(values, weights, preferred_element_type=F32)
        mixture, sums = both[:HD], both[HD : HD + 1]
        if not first:
            sums = old_refs[1][index : index + 1, :] * factor + sums
            mixture = old_refs[2][half, g] * factor + mixture
        if last:
            result = (mixture * (1.0 / sums)).astype(BF16).T
            for r in range(GQ):
                head = g * GQ + r
                out_ref[
                    half * half_tok : (half + 1) * half_tok, head * HD : (head + 1) * HD
                ] = result[r * half_tok : (r + 1) * half_tok]
        else:
            new_refs[0][index : index + 1, :] = top
            new_refs[1][index : index + 1, :] = sums
            new_refs[2][half, g] = mixture

    scores = scores_of(0)
    for g in range(KVH):
        upcoming = scores_of(g + 1) if g + 1 < KVH else None
        value_rows = jnp.concatenate(
            [gathered((KVH + g) * HD, 0), gathered((KVH + g) * HD, 1)], axis=0
        )
        values = jnp.concatenate([value_rows.T, ones], axis=0)
        update(0, g, scores[0], values[:, :keys_half])
        update(1, g, scores[1], values)
        scores = upcoming

    slot = slots_ref[me]
    head = slot // stride
    phase = slot % stride
    per_block = half_tok // stride
    peers = len(where)
    out_rows = 2 * per_block * peers
    row = lax.broadcasted_iota(jnp.int32, (out_rows, peers * half_tok), 0)
    lane = lax.broadcasted_iota(jnp.int32, (out_rows, peers * half_tok), 1)
    source = (row // (2 * per_block)) * half_tok + (row % (2 * per_block)) // 2 * stride + phase
    hit = source == lane
    pick_key = jnp.where(hit & (row % 2 == 0), 1.0, 0.0).astype(BF16)
    pick_value = jnp.where(hit & (row % 2 == 1), 1.0, 0.0).astype(BF16)
    key_col = pl.multiple_of(head * HD, HD)
    value_col = pl.multiple_of((KVH + head) * HD, HD)
    if not first:
        cache_ref[...] = old_cache_ref[...]
    for half in range(2):
        picked = jnp.dot(pick_key, gathered(key_col, half), preferred_element_type=F32)
        picked += jnp.dot(pick_value, gathered(value_col, half), preferred_element_type=F32)
        picked = picked.astype(BF16)
        for i, pair in enumerate(pair_of):
            block = pair if half == 0 else 2 * devices - 1 - pair
            cache_ref[block] = picked[i * 2 * per_block : (i + 1) * 2 * per_block]


def attend_chunk(pairs, slots, blocks, offsets, counts, queries, trig, state, last):
    devices = lax.axis_size("seq")
    tok_dev = blocks[0].shape[-2]
    stride = devices // KVH
    rows = GQ * tok_dev // 2
    first = state is None
    operands = [pairs, slots, *blocks]
    operands += [queries, trig] if first else list(state)
    outs = []
    if first:
        outs.append(jax.ShapeDtypeStruct((2, KVH, HD, rows), BF16))
    if last:
        outs.append(jax.ShapeDtypeStruct((tok_dev, QH * HD), BF16))
    else:
        outs += [jax.ShapeDtypeStruct((2 * KVH, rows), F32)] * 2
        outs.append(jax.ShapeDtypeStruct((2, KVH, HD, rows), F32))
    outs.append(jax.ShapeDtypeStruct((2 * devices, tok_dev // stride, HD), BF16))
    aliases = {}
    base = 2 + len(blocks)
    if not first:
        aliases = {base + 4: 1} if last else {base + 1 + i: i for i in range(4)}
    results = pl.pallas_call(
        functools.partial(chunk_kernel, devices, offsets, counts, first, last),
        out_shape=tuple(outs),
        in_specs=[SMEM_SPEC, SMEM_SPEC] + [VMEM_SPEC] * (len(operands) - 2),
        out_specs=tuple([VMEM_SPEC] * len(outs)),
        input_output_aliases=aliases,
        compiler_params=params(24),
        cost_estimate=pl.CostEstimate(
            flops=6 * len(offsets) * (tok_dev // 2) * rows * KVH * HD * 2 // 1,
            bytes_accessed=1 << 20,
            transcendentals=0,
        ),
        name="attend",
    )(*operands)
    if first or last:
        return tuple(results)
    return (state[0], *results)


def swap(x, offset):
    devices = lax.axis_size("seq")
    return lax.ppermute(x, "seq", [(s, s ^ offset) for s in range(devices)])


def layout_of(devices):
    cores = 2
    chips = devices // cores
    outer = 1 << -(-(chips.bit_length() - 1) // 2)
    return outer, chips // outer, cores


def whole_step(queries, keys, values, block_pairs, decode_slots):
    devices = lax.axis_size("seq")
    tok_dev = queries.shape[0]
    stride = devices // KVH
    outer, inner, cores = layout_of(devices)

    def hbm(x):
        return pltpu.with_memory_space_constraint(x, pltpu.HBM)

    kv, trig = prep(hbm(block_pairs), hbm(keys), hbm(values))
    plane = inner * cores
    far = [kv] + [swap(kv, step * plane) for step in range(1, outer)]
    chunks = []
    for step in range(outer):
        near = [far[step]]
        for y in range(1, inner):
            near.append(swap(far[step], y * cores))
        pair = swap(jnp.stack(near), 1)
        offsets = tuple(
            step * plane + y * cores + core for core in range(cores) for y in range(inner)
        )
        chunks.append((near + [pair], offsets, tuple([0] * inner + [inner])))
    groups = [chunks[:1], chunks[1:-1], chunks[-1:]]
    state = None
    for index, group in enumerate(groups):
        state = attend_chunk(
            block_pairs,
            decode_slots,
            [block for chunk in group for block in chunk[0]],
            tuple(offset for chunk in group for offset in chunk[1]),
            tuple(count for chunk in group for count in chunk[2]),
            queries,
            trig,
            state,
            index == len(groups) - 1,
        )
    attended, cache = state
    return attended, cache.reshape(1, tok_dev * devices // stride, 2, HD)


def solution(mesh):
    placed = (
        P(("groups", "seq"), None),
        P(("groups", "seq"), None),
        P(("groups", "seq"), None),
        P("groups"),
        P("groups"),
    )
    return jax.shard_map(
        whole_step,
        mesh=mesh,
        in_specs=placed,
        out_specs=(P(("groups", "seq"), None), P(("groups", "seq"), None, None, None)),
        check_vma=False,
    )
```

profile of v0, /device:TPU:0, one launch (start us, length us, event | category | flops | bytes accessed | tf_op | source)
XLA Modules:
  0.0 32.7 jit_solution(4525170123017237170)
XLA Ops:
  0.6 1.0 %prep.1 = (bf16[64,1024]{1,0:T(8,128)(2,1)S(1)}, f32[64,256]{1,0:T(8,128)S(1)}) custom-call(s32[16]{0:T(128)} %refs_0_.5, bf16[64,512]{1,0:T(8,128)(2,1)} %k_hbm.1, bf16[64,512]{1,0:T(8,128)(2,1)} %v_hbm.1), custom_call_target="tpu_custom_call" | custom-call | tf_op jit(solution)/shard_map/prep/pallas_call | solution.py:76
  1.6 4.1 %collective-permute-start.8 = (bf16[64,1024]{1,0:T(8,128)(2,1)S(1)}, bf16[64,1024]{1,0:T(8,128)(2,1)S(1)}, u32[]{:S(2)}, u32[]{:S(2)}) collective-permute-start(bf16[64,1024]{1,0:T(8,128)(2,1)S(1)} %get-tuple-element.15.refs_2_), channel_id=1, source_target_pairs={{0,8},{1,9},{2,10},{3,11},{4,12},{5,13},{6,14},{7,15},{8,0},{9,1},... | collective-permute-start | bytes 393224 | tf_op jit(solution)/shard_map/ppermute | solution.py:277
  5.7 1.6 %collective-permute-start.5 = (bf16[64,1024]{1,0:T(8,128)(2,1)S(1)}, bf16[64,1024]{1,0:T(8,128)(2,1)S(1)}, u32[]{:S(2)}, u32[]{:S(2)}) collective-permute-start(bf16[64,1024]{1,0:T(8,128)(2,1)S(1)} %get-tuple-element.15.refs_2_), channel_id=1, source_target_pairs={{0,4},{1,5},{2,6},{3,7},{4,0},{5,1},{6,2},{7,3},{8,12},{9,13},{10,... | collective-permute-start | bytes 393224 | tf_op jit(solution)/shard_map/ppermute | solution.py:277
  7.3 1.5 %collective-permute-start.3 = (bf16[64,1024]{1,0:T(8,128)(2,1)S(1)}, bf16[64,1024]{1,0:T(8,128)(2,1)S(1)}, u32[]{:S(2)}, u32[]{:S(2)}) collective-permute-start(bf16[64,1024]{1,0:T(8,128)(2,1)S(1)} %get-tuple-element.15.refs_2_), channel_id=1, source_target_pairs={{0,2},{1,3},{2,0},{3,1},{4,6},{5,7},{6,4},{7,5},{8,10},{9,11},{10,... | collective-permute-start | bytes 393224 | tf_op jit(solution)/shard_map/ppermute | solution.py:277
  8.8 0.2 collective-permute-start
  9.0 4.5 %collective-permute-done.8.refs_5_ = bf16[64,1024]{1,0:T(8,128)(2,1)S(1)} collective-permute-done((bf16[64,1024]{1,0:T(8,128)(2,1)S(1)}, bf16[64,1024]{1,0:T(8,128)(2,1)S(1)}, u32[]{:S(2)}, u32[]{:S(2)}) %collective-permute-start.8) | collective-permute-done | bytes 131104 | tf_op jit(solution)/shard_map/ppermute | solution.py:277
  13.6 2.3 %collective-permute-start.9 = (bf16[64,1024]{1,0:T(8,128)(2,1)S(1)}, bf16[64,1024]{1,0:T(8,128)(2,1)S(1)}, u32[]{:S(2)}, u32[]{:S(2)}) collective-permute-start(bf16[64,1024]{1,0:T(8,128)(2,1)S(1)} %collective-permute-done.8.refs_5_), channel_id=1, source_target_pairs={{0,2},{1,3},{2,0},{3,1},{4,6},{5,7},{6,4},{7,5},{8,10},{9,11},{10,... | collective-permute-start | bytes 393224 | tf_op jit(solution)/shard_map/ppermute | solution.py:277
  15.8 0.0 collective-permute-done.5.refs_2_
  15.8 0.0 collective-permute-start.6
  15.8 0.0 collective-permute-done.3.refs_3_
  15.9 0.1 collective-permute-start.4
  15.9 0.1 collective-permute-done.refs_2_
  16.1 2.0 %collective-permute-start.1 = (bf16[64,1024]{1,0:T(8,128)(2,1)S(1)}, bf16[64,1024]{1,0:T(8,128)(2,1)S(1)}, u32[]{:S(2)}, u32[]{:S(2)}) collective-permute-start(bf16[64,1024]{1,0:T(8,128)(2,1)S(1)} %collective-permute-done.refs_2_), channel_id=1, source_target_pairs={{0,2},{1,3},{2,0},{3,1},{4,6},{5,7},{6,4},{7,5},{8,10},{9,11},{10,... | collective-permute-start | bytes 393224 | tf_op jit(solution)/shard_map/ppermute | solution.py:277
  18.0 0.7 %collective-permute-done.9.refs_6_ = bf16[64,1024]{1,0:T(8,128)(2,1)S(1)} collective-permute-done((bf16[64,1024]{1,0:T(8,128)(2,1)S(1)}, bf16[64,1024]{1,0:T(8,128)(2,1)S(1)}, u32[]{:S(2)}, u32[]{:S(2)}) %collective-permute-start.9) | collective-permute-done | bytes 131104 | tf_op jit(solution)/shard_map/ppermute | solution.py:277
  18.8 0.1 collective-permute-start.10
  18.9 3.2 %collective-permute-done.6.refs_3_ = bf16[64,1024]{1,0:T(8,128)(2,1)S(1)} collective-permute-done((bf16[64,1024]{1,0:T(8,128)(2,1)S(1)}, bf16[64,1024]{1,0:T(8,128)(2,1)S(1)}, u32[]{:S(2)}, u32[]{:S(2)}) %collective-permute-start.6) | collective-permute-done | bytes 131104 | tf_op jit(solution)/shard_map/ppermute | solution.py:277
  22.1 0.0 copy-start
  22.1 0.1 collective-permute-start.7
  22.2 1.3 %collective-permute-done.1.refs_3_ = bf16[64,1024]{1,0:T(8,128)(2,1)S(1)} collective-permute-done((bf16[64,1024]{1,0:T(8,128)(2,1)S(1)}, bf16[64,1024]{1,0:T(8,128)(2,1)S(1)}, u32[]{:S(2)}, u32[]{:S(2)}) %collective-permute-start.1) | collective-permute-done | bytes 131104 | tf_op jit(solution)/shard_map/ppermute | solution.py:277
  23.5 0.0 copy-start.1
  23.6 0.0 copy-start.2
  23.6 0.1 collective-permute-start.2
  23.7 0.0 collective-permute-done.4.refs_4_
  23.7 0.0 copy-done
  23.7 0.5 %copy-done.1 = s32[16]{0:T(128)S(1)} copy-done((s32[16]{0:T(128)S(1)}, s32[16]{0:T(128)}, u32[]{:S(2)}) %copy-start.1) | copy-done | bytes 88
  24.2 0.0 copy-done.2
  24.2 2.4 %attend.3 = (bf16[2,4,128,256]{3,2,1,0:T(8,128)(2,1)S(1)}, f32[8,256]{1,0:T(8,128)S(1)}, f32[8,256]{1,0:T(8,128)S(1)}, f32[2,4,128,256]{3,2,1,0:T(8,128)S(1)}, bf16[32,16,128]{2,1,0:T(8,128)(2,1)}) custom-call(s32[16]{0:T(128)S(1)} %copy-done.1, s32[16]{0:T(128)S(1)} %copy-done.2, bf16[64,1024]{1,0:T(8,128)(2,1)S(1)} %get-tuple-element.15.refs_2_, ...), custom_call_target="tpu_custom_call" | custom-call | flops 201326592 | bytes 1048576 | tf_op jit(solution)/shard_map/attend/pallas_call | solution.py:256
  26.6 0.0 collective-permute-done.10.refs_7_
  26.6 0.0 collective-permute-done.7.refs_4_
  26.6 3.4 %attend.4 = (f32[8,256]{1,0:T(8,128)S(1)}, f32[8,256]{1,0:T(8,128)S(1)}, f32[2,4,128,256]{3,2,1,0:T(8,128)S(1)}, bf16[32,16,128]{2,1,0:T(8,128)(2,1)}) custom-call(s32[16]{0:T(128)S(1)} %copy-done.1, s32[16]{0:T(128)S(1)} %copy-done.2, ...), custom_call_target="tpu_custom_call", output_to_operand_aliasing={{0}: (9, {}), {1}: (10, {}), {2}: (11, {}), {3}: (12, {})} | custom-call | flops 402653184 | bytes 1048576 | tf_op jit(solution)/shard_map/attend/pallas_call | solution.py:256
  30.0 0.0 collective-permute-done.2.refs_4_
  30.0 2.7 %attend.5 = (bf16[64,4096]{1,0:T(8,128)(2,1)}, bf16[32,16,128]{2,1,0:T(8,128)(2,1)}) custom-call(s32[16]{0:T(128)S(1)} %copy-done.1, s32[16]{0:T(128)S(1)} %copy-done.2, bf16[64,1024]{1,0:T(8,128)(2,1)S(1)} %collective-permute-done.refs_2_, bf16[64,1024]{1,0:T(8,128)(2,1)S(1)} %collective-permute-done.1.refs_3_, ...), custom_call_target="tpu_custom_call", output_to_operand_aliasing={{1}: (9, {})} | custom-call | flops 201326592 | bytes 1048576 | tf_op jit(solution)/shard_map/attend/pallas_call | solution.py:256
  (4 shorter events, 0.1 us)
Async XLA Ops:
  1.6 12.0 %collective-permute-start.8 = (bf16[64,1024]{1,0:T(8,128)(2,1)S(1)}, bf16[64,1024]{1,0:T(8,128)(2,1)S(1)}, u32[]{:S(2)}, u32[]{:S(2)}) collective-permute-start(bf16[64,1024]{1,0:T(8,128)(2,1)S(1)} %get-tuple-element.15.refs_2_), channel_id=1, source_target_pairs={{0,8},{1,9},{2,10},{3,11},{4,12},{5,13},{6,14},{7,15},{8,0},{9,1},... | collective-permute-start | bytes 393224 | tf_op jit(solution)/shard_map/ppermute | solution.py:277
  5.7 10.1 %collective-permute-start.5 = (bf16[64,1024]{1,0:T(8,128)(2,1)S(1)}, bf16[64,1024]{1,0:T(8,128)(2,1)S(1)}, u32[]{:S(2)}, u32[]{:S(2)}) collective-permute-start(bf16[64,1024]{1,0:T(8,128)(2,1)S(1)} %get-tuple-element.15.refs_2_), channel_id=1, source_target_pairs={{0,4},{1,5},{2,6},{3,7},{4,0},{5,1},{6,2},{7,3},{8,12},{9,13},{10,... | collective-permute-start | bytes 393224 | tf_op jit(solution)/shard_map/ppermute | solution.py:277
  7.3 8.5 %collective-permute-start.3 = (bf16[64,1024]{1,0:T(8,128)(2,1)S(1)}, bf16[64,1024]{1,0:T(8,128)(2,1)S(1)}, u32[]{:S(2)}, u32[]{:S(2)}) collective-permute-start(bf16[64,1024]{1,0:T(8,128)(2,1)S(1)} %get-tuple-element.15.refs_2_), channel_id=1, source_target_pairs={{0,2},{1,3},{2,0},{3,1},{4,6},{5,7},{6,4},{7,5},{8,10},{9,11},{10,... | collective-permute-start | bytes 393224 | tf_op jit(solution)/shard_map/ppermute | solution.py:277
  8.8 7.2 %collective-permute-start = (bf16[64,1024]{1,0:T(8,128)(2,1)S(1)}, bf16[64,1024]{1,0:T(8,128)(2,1)S(1)}, u32[]{:S(2)}, u32[]{:S(2)}) collective-permute-start(bf16[64,1024]{1,0:T(8,128)(2,1)S(1)} %get-tuple-element.15.refs_2_), channel_id=1, source_target_pairs={{0,12},{1,13},{2,14},{3,15},{4,8},{5,9},{6,10},{7,11},{8,4},{9,5},... | collective-permute-start | bytes 393224 | tf_op jit(solution)/shard_map/ppermute | solution.py:277
  13.6 5.2 %collective-permute-start.9 = (bf16[64,1024]{1,0:T(8,128)(2,1)S(1)}, bf16[64,1024]{1,0:T(8,128)(2,1)S(1)}, u32[]{:S(2)}, u32[]{:S(2)}) collective-permute-start(bf16[64,1024]{1,0:T(8,128)(2,1)S(1)} %collective-permute-done.8.refs_5_), channel_id=1, source_target_pairs={{0,2},{1,3},{2,0},{3,1},{4,6},{5,7},{6,4},{7,5},{8,10},{9,11},{10,... | collective-permute-start | bytes 393224 | tf_op jit(solution)/shard_map/ppermute | solution.py:277
  15.8 6.3 %collective-permute-start.6 = (bf16[64,1024]{1,0:T(8,128)(2,1)S(1)}, bf16[64,1024]{1,0:T(8,128)(2,1)S(1)}, u32[]{:S(2)}, u32[]{:S(2)}) collective-permute-start(bf16[64,1024]{1,0:T(8,128)(2,1)S(1)} %collective-permute-done.5.refs_2_), channel_id=1, source_target_pairs={{0,2},{1,3},{2,0},{3,1},{4,6},{5,7},{6,4},{7,5},{8,10},{9,11},{10,... | collective-permute-start | bytes 393224 | tf_op jit(solution)/shard_map/ppermute | solution.py:277
  15.9 7.8 %collective-permute-start.4 = (bf16[2,64,1024]{2,1,0:T(8,128)(2,1)S(1)}, bf16[2,64,1024]{2,1,0:T(8,128)(2,1)S(1)}, u32[]{:S(2)}, u32[]{:S(2)}) collective-permute-start(bf16[2,64,1024]{2,1,0:T(8,128)(2,1)S(1)} %pad_maximum_fusion.1), channel_id=1, source_target_pairs={{0,1},{1,0},{2,3},{3,2},{4,5},{5,4},{6,7},{7,6},{8,9},{9,8},{10,11... | collective-permute-start | bytes 786440 | tf_op jit(solution)/shard_map/ppermute | solution.py:277
  16.1 7.5 %collective-permute-start.1 = (bf16[64,1024]{1,0:T(8,128)(2,1)S(1)}, bf16[64,1024]{1,0:T(8,128)(2,1)S(1)}, u32[]{:S(2)}, u32[]{:S(2)}) collective-permute-start(bf16[64,1024]{1,0:T(8,128)(2,1)S(1)} %collective-permute-done.refs_2_), channel_id=1, source_target_pairs={{0,2},{1,3},{2,0},{3,1},{4,6},{5,7},{6,4},{7,5},{8,10},{9,11},{10,... | collective-permute-start | bytes 393224 | tf_op jit(solution)/shard_map/ppermute | solution.py:277
  18.8 7.8 %collective-permute-start.10 = (bf16[2,64,1024]{2,1,0:T(8,128)(2,1)S(1)}, bf16[2,64,1024]{2,1,0:T(8,128)(2,1)S(1)}, u32[]{:S(2)}, u32[]{:S(2)}) collective-permute-start(bf16[2,64,1024]{2,1,0:T(8,128)(2,1)S(1)} %pad_maximum_fusion.3), channel_id=1, source_target_pairs={{0,1},{1,0},{2,3},{3,2},{4,5},{5,4},{6,7},{7,6},{8,9},{9,8},{10,11... | collective-permute-start | bytes 786440 | tf_op jit(solution)/shard_map/ppermute | solution.py:277
  22.1 1.6 %copy-start = (bf16[64,4096]{1,0:T(8,128)(2,1)S(1)}, bf16[64,4096]{1,0:T(8,128)(2,1)}, u32[]{:S(2)}) copy-start(bf16[64,4096]{1,0:T(8,128)(2,1)} %refs_5_.1) | copy-start | bytes 1572868
  22.1 4.4 %collective-permute-start.7 = (bf16[2,64,1024]{2,1,0:T(8,128)(2,1)S(1)}, bf16[2,64,1024]{2,1,0:T(8,128)(2,1)S(1)}, u32[]{:S(2)}, u32[]{:S(2)}) collective-permute-start(bf16[2,64,1024]{2,1,0:T(8,128)(2,1)S(1)} %pad_maximum_fusion.2), channel_id=1, source_target_pairs={{0,1},{1,0},{2,3},{3,2},{4,5},{5,4},{6,7},{7,6},{8,9},{9,8},{10,11... | collective-permute-start | bytes 786440 | tf_op jit(solution)/shard_map/ppermute | solution.py:277
  23.5 0.7 %copy-start.1 = (s32[16]{0:T(128)S(1)}, s32[16]{0:T(128)}, u32[]{:S(2)}) copy-start(s32[16]{0:T(128)} %refs_0_.5) | copy-start | bytes 196
  23.6 0.7 %copy-start.2 = (s32[16]{0:T(128)S(1)}, s32[16]{0:T(128)}, u32[]{:S(2)}) copy-start(s32[16]{0:T(128)} %refs_1_.5) | copy-start | bytes 196
  23.6 6.4 %collective-permute-start.2 = (bf16[2,64,1024]{2,1,0:T(8,128)(2,1)S(1)}, bf16[2,64,1024]{2,1,0:T(8,128)(2,1)S(1)}, u32[]{:S(2)}, u32[]{:S(2)}) collective-permute-start(bf16[2,64,1024]{2,1,0:T(8,128)(2,1)S(1)} %pad_maximum_fusion), channel_id=1, source_target_pairs={{0,1},{1,0},{2,3},{3,2},{4,5},{5,4},{6,7},{7,6},{8,9},{9,8},{10,11... | collective-permute-start | bytes 786440 | tf_op jit(solution)/shard_map/ppermute | solution.py:277
where the time goes:
time: 32.9 us; the launch traced here: 32.7 us
  starting transfers between devices  12 us (36%)
  waiting for transfers between devices  9.89 us (30%)
  Pallas kernels  9.41 us (29%)
  between operations  0.73 us (2%)
  local copies, waits for them, and re-layouts  0.56 us (2%)
    ppermute x11, starting transfers between devices, swap(): return lax.ppermute(x, 'seq', [(s, s ^ offset) for s in range(devices)])  12 us
    ppermute x11, waiting for transfers between devices, swap(): return lax.ppermute(x, 'seq', [(s, s ^ offset) for s in range(devices)])  9.89 us
    pallas_call x3, Pallas kernels, attend_chunk(): pl.pallas_call(functools.partial(chunk_kernel, devices, offsets, counts,...  8.45 us
    pallas_call x1, Pallas kernels, prep(): pl.pallas_call(functools.partial(prep_kernel, devices), out_shape=(jax.Sh...  0.96 us
  transfers between devices with their start and end apart: 11, of which 5 were waited for; matrix products, arithmetic and copies ran while one was open for 0% of the time, Pallas kernels for 18%

commit v1 on v0

v1 whole, which is shorter than its diff:
```python
import functools
import math

import jax
import jax.numpy as jnp
from jax import lax
from jax.experimental import pallas as pl
from jax.experimental.pallas import tpu as pltpu
from jax.sharding import PartitionSpec as P


HD = 128
KVH = 4
GQ = 8
QH = 32

ROPE_BASE = 500000.0
NEGATIVE = -1e30
LOG2E = math.log2(math.e)

VMEM_SPEC = pl.BlockSpec(memory_space=pltpu.VMEM)
HBM_SPEC = pl.BlockSpec(memory_space=pltpu.HBM)
F32 = jnp.float32
BF16 = jnp.bfloat16


def params(mib):
    return pltpu.CompilerParams(vmem_limit_bytes=mib << 20)


def rotation_tables(block, devices, tok_dev):
    half_tok = tok_dev // 2
    row = lax.broadcasted_iota(jnp.int32, (tok_dev, HD), 0)
    lane = lax.broadcasted_iota(jnp.int32, (tok_dev, HD), 1)
    early = row < half_tok
    position = jnp.where(
        early, block * half_tok + row, (2 * devices - 1 - block) * half_tok + row - half_tok
    )
    low = lane < HD // 2
    index = jnp.where(low, lane, lane - HD // 2).astype(F32)
    frequency = jnp.exp(index * (-2.0 * math.log(ROPE_BASE) / HD))
    angle = position.astype(F32) * frequency
    sine = jnp.sin(angle)
    return jnp.cos(angle), jnp.where(low, -sine, sine)


def turn(block, cosine, sine):
    wide = block.astype(F32)
    return (wide * cosine + pltpu.roll(wide, HD // 2, 1) * sine).astype(BF16)


def prep_kernel(
    devices, pairs_hbm, slots_hbm, k_hbm, v_hbm, kv_ref, trig_ref, info_ref, pairs_ref, slots_ref, k_ref, sems
):
    tok_dev = k_ref.shape[0]
    width = KVH * HD
    stride = devices // KVH
    copies = [
        pltpu.make_async_copy(pairs_hbm, pairs_ref, sems.at[0]),
        pltpu.make_async_copy(k_hbm, k_ref, sems.at[1]),
        pltpu.make_async_copy(v_hbm, kv_ref.at[:, width:], sems.at[2]),
        pltpu.make_async_copy(slots_hbm, slots_ref, sems.at[3]),
    ]
    for copy in copies:
        copy.start()
    me = lax.axis_index("seq")
    copies[0].wait()
    cosine, sine = rotation_tables(pairs_ref[me], devices, tok_dev)
    trig_ref[:, :HD] = cosine
    trig_ref[:, HD:] = sine
    copies[1].wait()
    for g in range(KVH):
        cols = slice(g * HD, (g + 1) * HD)
        kv_ref[:, cols] = turn(k_ref[:, cols], cosine, sine)
    lane = lax.broadcasted_iota(jnp.int32, (1, devices), 1)
    peers = jnp.zeros((1, devices), jnp.int32)
    for i in range(devices):
        peers = jnp.where(lane == i, pairs_ref[lax.bitwise_xor(me, i)], peers)
    copies[3].wait()
    slot = slots_ref[me]
    info_ref[0:1, :] = peers
    info_ref[1:2, :] = jnp.where(lane == 0, slot // stride, slot % stride)
    copies[2].wait()


def prep(pairs, slots, keys, values):
    devices = lax.axis_size("seq")
    tok_dev = keys.shape[0]
    return pl.pallas_call(
        functools.partial(prep_kernel, devices),
        out_shape=(
            jax.ShapeDtypeStruct((tok_dev, 2 * KVH * HD), BF16),
            jax.ShapeDtypeStruct((tok_dev, 2 * HD), F32),
            jax.ShapeDtypeStruct((2, devices), jnp.int32),
        ),
        in_specs=[HBM_SPEC] * 4,
        out_specs=(VMEM_SPEC,) * 3,
        scratch_shapes=[
            pltpu.SMEM(pairs.shape, jnp.int32),
            pltpu.SMEM(slots.shape, jnp.int32),
            pltpu.VMEM(keys.shape, BF16),
            pltpu.SemaphoreType.DMA((4,)),
        ],
        compiler_params=params(8),
        name="prep",
    )(pairs, slots, keys, values)


def turn_kernel(q_hbm, trig_ref, turned_ref, q_ref, sems):
    tok_dev = q_ref.shape[0]
    half_tok = tok_dev // 2
    width = GQ * HD
    copies = []
    for g in range(KVH):
        cols = pl.ds(g * width, width)
        copies.append(pltpu.make_async_copy(q_hbm.at[:, cols], q_ref.at[:, cols], sems.at[g]))
        copies[g].start()
    cosine, sine = trig_ref[:, :HD], trig_ref[:, HD:]
    for g in range(KVH):
        copies[g].wait()
        turned = [
            turn(q_ref[:, head * HD : (head + 1) * HD], cosine, sine)
            for head in range(g * GQ, (g + 1) * GQ)
        ]
        for half in range(2):
            part = [t[half * half_tok : (half + 1) * half_tok] for t in turned]
            turned_ref[half, g] = jnp.concatenate(part, axis=0).T


def turn_queries(queries, trig):
    rows = GQ * queries.shape[0] // 2
    return pl.pallas_call(
        turn_kernel,
        out_shape=jax.ShapeDtypeStruct((2, KVH, HD, rows), BF16),
        in_specs=[HBM_SPEC, VMEM_SPEC],
        out_specs=VMEM_SPEC,
        scratch_shapes=[pltpu.VMEM(queries.shape, BF16), pltpu.SemaphoreType.DMA((KVH,))],
        compiler_params=params(8),
        name="turn",
    )(queries, trig)


def fold(x):
    return x.reshape(x.shape[0] // 8, 8, x.shape[1])


def spread_max(x):
    for shift in (4, 2, 1):
        x = jnp.maximum(x, pltpu.roll(x, shift, 0))
    return x


def chunk_kernel(devices, offsets, counts, first, last, *refs):
    refs = list(refs)
    info_ref, turned_ref = refs.pop(0), refs.pop(0)
    block_refs = [refs.pop(0) for _ in counts]
    if not first:
        old_refs = [refs.pop(0) for _ in range(3)]
        old_cache_ref = refs.pop(0)
    if last:
        out_hbm, cache_hbm, out_ref, cache_ref, sems = refs
    else:
        new_refs = [refs.pop(0) for _ in range(3)]
        cache_ref = refs.pop(0)

    own = info_ref[0, 0]
    head, phase = info_ref[1, 0], info_ref[1, 1]
    tok_dev = block_refs[0].shape[-2]
    half_tok = tok_dev // 2
    stride = devices // KVH
    rows = GQ * half_tok

    where = []
    for ref, count in zip(block_refs, counts):
        where += [ref.at[i] for i in range(count)] if count else [ref]
    pair_of = [info_ref[0, offset] for offset in offsets]

    def gathered(col, half):
        return jnp.concatenate(
            [w[half * half_tok : (half + 1) * half_tok, pl.ds(col, HD)] for w in where], axis=0
        )

    per_block = half_tok // stride
    peers = len(where)
    out_rows = 2 * per_block * peers
    row = lax.broadcasted_iota(jnp.int32, (out_rows, peers * half_tok), 0)
    lane = lax.broadcasted_iota(jnp.int32, (out_rows, peers * half_tok), 1)
    source = (row // (2 * per_block)) * half_tok + (row % (2 * per_block)) // 2 * stride + phase
    hit = source == lane
    pick_key = jnp.where(hit & (row % 2 == 0), 1.0, 0.0).astype(BF16)
    pick_value = jnp.where(hit & (row % 2 == 1), 1.0, 0.0).astype(BF16)
    key_col = pl.multiple_of(head * HD, HD)
    value_col = pl.multiple_of((KVH + head) * HD, HD)
    if not first:
        cache_ref[...] = old_cache_ref[...]
    for half in range(2):
        picked = jnp.dot(pick_key, gathered(key_col, half), preferred_element_type=F32)
        picked += jnp.dot(pick_value, gathered(value_col, half), preferred_element_type=F32)
        picked = picked.astype(BF16)
        for i, pair in enumerate(pair_of):
            block = pair if half == 0 else 2 * devices - 1 - pair
            cache_ref[block] = picked[i * 2 * per_block : (i + 1) * 2 * per_block]
    copies = []
    if last:
        copies.append(pltpu.make_async_copy(cache_ref, cache_hbm, sems.at[KVH]))
        copies[0].start()

    scale = LOG2E / math.sqrt(HD)
    keys_half = len(where) * half_tok

    row = lax.broadcasted_iota(jnp.int32, (half_tok, HD), 0)
    lane = lax.broadcasted_iota(jnp.int32, (half_tok, HD), 1)

    def key_flags(distance):
        column = jnp.where(distance == 0, row, jnp.where(distance < 0, half_tok, HD))
        return jnp.where(lane == column, 1.0, 0.0).astype(BF16)

    early_flags = jnp.concatenate([key_flags(own - pair) for pair in pair_of], axis=0)
    late_flags = jnp.concatenate([key_flags(pair - own) for pair in pair_of], axis=0)
    blank = jnp.zeros((keys_half, HD), BF16)
    order = lax.broadcasted_iota(jnp.int32, (HD, rows), 0)
    token = lax.broadcasted_iota(jnp.int32, (HD, rows), 1) % half_tok
    barred = jnp.where((order > token) & (order <= half_tok), NEGATIVE, 0.0).astype(BF16)
    ones = jnp.ones((16, 2 * keys_half), BF16)

    def scores_of(g):
        key_early, key_late = gathered(g * HD, 0), gathered(g * HD, 1)
        query_early = jnp.concatenate([turned_ref[0, g], barred], axis=0)
        query_late = jnp.concatenate([turned_ref[1, g], barred], axis=0)
        early = jnp.dot(
            jnp.concatenate([key_early, early_flags], axis=1),
            query_early,
            preferred_element_type=F32,
        )
        late_keys = jnp.concatenate([key_early, key_late], axis=0)
        flags = jnp.concatenate([blank, late_flags], axis=0)
        late = jnp.dot(
            jnp.concatenate([late_keys, flags], axis=1), query_late, preferred_element_type=F32
        )
        return early, late

    def update(half, g, scores, values):
        index = half * KVH + g
        scores = fold(scores)
        top = spread_max(jnp.max(scores, axis=0)) * scale
        if not first:
            old_max = old_refs[0][index]
            top = jnp.maximum(old_max, top)
            factor = jnp.exp2(old_max - top)
        weights = jnp.exp2(scores * scale - top[None]).astype(BF16).reshape(-1, rows)
        both = jnp.dot(values, weights, preferred_element_type=F32)
        mixture, sums = fold(both[:HD]), both[HD : HD + 8]
        if not first:
            sums = old_refs[1][index] * factor + sums
            mixture = fold(old_refs[2][half, g]) * factor[None] + mixture
        if last:
            result = (mixture * (1.0 / sums)[None]).reshape(HD, rows).astype(BF16).T
            for r in range(GQ):
                col = (g * GQ + r) * HD
                out_ref[half * half_tok : (half + 1) * half_tok, col : col + HD] = result[
                    r * half_tok : (r + 1) * half_tok
                ]
        else:
            new_refs[0][index] = top
            new_refs[1][index] = sums
            new_refs[2][half, g] = mixture.reshape(HD, rows)

    scores = [scores_of(g) for g in range(KVH)]
    values = []
    for g in range(KVH):
        value_rows = jnp.concatenate(
            [gathered((KVH + g) * HD, 0), gathered((KVH + g) * HD, 1)], axis=0
        )
        values.append(jnp.concatenate([value_rows.T, ones], axis=0))
    for g in range(KVH):
        update(0, g, scores[g][0], values[g][:, :keys_half])
        update(1, g, scores[g][1], values[g])
        if last:
            cols = pl.ds(g * GQ * HD, GQ * HD)
            copies.append(
                pltpu.make_async_copy(out_ref.at[:, cols], out_hbm.at[:, cols], sems.at[g])
            )
            copies[-1].start()
    for copy in copies:
        copy.wait()


def attend_chunk(info, turned, blocks, offsets, counts, state, last):
    devices = lax.axis_size("seq")
    tok_dev = blocks[0].shape[-2]
    stride = devices // KVH
    rows = GQ * tok_dev // 2
    first = state is None
    operands = [info, turned, *blocks, *(state or ())]
    cache = jax.ShapeDtypeStruct((2 * devices, tok_dev // stride, HD), BF16)
    aliases, scratch = {}, []
    if last:
        out = jax.ShapeDtypeStruct((tok_dev, QH * HD), BF16)
        outs = (out, cache)
        scratch = [
            pltpu.VMEM(out.shape, BF16),
            pltpu.VMEM(cache.shape, BF16),
            pltpu.SemaphoreType.DMA((KVH + 1,)),
        ]
    else:
        small = jax.ShapeDtypeStruct((2 * KVH, 8, rows), F32)
        outs = (small, small, jax.ShapeDtypeStruct((2, KVH, HD, rows), F32), cache)
        if not first:
            aliases = {2 + len(blocks) + i: i for i in range(4)}
    work = len(offsets) * (tok_dev // 2) * rows * KVH * HD
    return pl.pallas_call(
        functools.partial(chunk_kernel, devices, offsets, counts, first, last),
        out_shape=outs,
        in_specs=[VMEM_SPEC] * len(operands),
        out_specs=tuple([HBM_SPEC if last else VMEM_SPEC] * len(outs)),
        scratch_shapes=scratch,
        input_output_aliases=aliases,
        compiler_params=params(24),
        cost_estimate=pl.CostEstimate(flops=12 * work, bytes_accessed=1 << 20, transcendentals=0),
        name="attend",
    )(*operands)


def swap(x, offset):
    devices = lax.axis_size("seq")
    return lax.ppermute(x, "seq", [(s, s ^ offset) for s in range(devices)])


def layout_of(devices):
    cores = 2
    chips = devices // cores
    outer = 1 << -(-(chips.bit_length() - 1) // 2)
    return outer, chips // outer, cores


def whole_step(queries, keys, values, block_pairs, decode_slots):
    devices = lax.axis_size("seq")
    tok_dev = queries.shape[0]
    stride = devices // KVH
    outer, inner, cores = layout_of(devices)

    def hbm(x):
        return pltpu.with_memory_space_constraint(x, pltpu.HBM)

    kv, trig, info = prep(hbm(block_pairs), hbm(decode_slots), hbm(keys), hbm(values))
    turned = turn_queries(hbm(queries), trig)
    plane = inner * cores
    far = [kv] + [swap(kv, step * plane) for step in range(1, outer)]
    chunks = []
    for step in range(outer):
        near = [far[step]]
        for y in range(1, inner):
            near.append(swap(far[step], y * cores))
        pair = swap(jnp.stack(near), 1)
        offsets = tuple(
            step * plane + y * cores + core for core in range(cores) for y in range(inner)
        )
        chunks.append((near + [pair], offsets, tuple([0] * inner + [inner])))
    state = None
    for step, (blocks, offsets, counts) in enumerate(chunks):
        state = attend_chunk(info, turned, blocks, offsets, counts, state, step == outer - 1)
    attended, cache = state
    return attended, cache.reshape(1, tok_dev * devices // stride, 2, HD)


def solution(mesh):
    placed = (
        P(("groups", "seq"), None),
        P(("groups", "seq"), None),
        P(("groups", "seq"), None),
        P("groups"),
        P("groups"),
    )
    return jax.shard_map(
        whole_step,
        mesh=mesh,
        in_specs=placed,
        out_specs=(P(("groups", "seq"), None), P(("groups", "seq"), None, None, None)),
        check_vma=False,
    )
```

time: 32.9 us -> 32 us (0.973)
  Pallas kernels: 9.41 us -> 7.46 us
  waiting for transfers between devices: 9.89 us -> 11.8 us
  local copies, waits for them, and re-layouts: 0.56 us -> 0 us
    pallas_call x3 -> x4, Pallas kernels: 8.45 us -> 4.8 us  [attend_chunk(): pl.pallas_call(functools.partial(chunk_kernel, devices, offsets, counts,...]
    ppermute x11, waiting for transfers between devices: 9.89 us -> 11.8 us  [swap(): return lax.ppermute(x, 'seq', [(s, s ^ offset) for s in range(devices)])]
    pallas_call x0 -> x1, Pallas kernels: none -> 1.66 us  [turn_queries(): pl.pallas_call(turn_kernel, out_shape=jax.ShapeDtypeStruct((2, KVH, HD, r...]
    unnamed x6 -> x0, local copies, waits for them, and re-layouts: 0.56 us -> none
  transfers between devices with their start and end apart: 11 -> 11, of which waited for: 5 -> 4; matrix products, arithmetic and copies ran while one was open for 0% -> 0% of each run, Pallas kernels for 18% -> 15%
where the time goes in v1:
time: 32 us; the launch traced here: 31.8 us
  waiting for transfers between devices  11.8 us (37%)
  starting transfers between devices  11.7 us (37%)
  Pallas kernels  7.46 us (23%)
  between operations  0.76 us (2%)
    ppermute x11, waiting for transfers between devices, swap(): return lax.ppermute(x, 'seq', [(s, s ^ offset) for s in range(devices)])  11.8 us
    ppermute x11, starting transfers between devices, swap(): return lax.ppermute(x, 'seq', [(s, s ^ offset) for s in range(devices)])  11.7 us
    pallas_call x4, Pallas kernels, attend_chunk(): pl.pallas_call(functools.partial(chunk_kernel, devices, offsets, counts,...  4.8 us
    pallas_call x1, Pallas kernels, turn_queries(): pl.pallas_call(turn_kernel, out_shape=jax.ShapeDtypeStruct((2, KVH, HD, r...  1.66 us
    pallas_call x1, Pallas kernels, prep(): pl.pallas_call(functools.partial(prep_kernel, devices), out_shape=(jax.Sh...  0.99 us
  transfers between devices with their start and end apart: 11, of which 4 were waited for; matrix products, arithmetic and copies ran while one was open for 0% of the time, Pallas kernels for 15%

profile of v1, /device:TPU:0, one launch (start us, length us, event | category | flops | bytes accessed | tf_op | source)
XLA Modules:
  0.0 31.8 jit_solution(13922394203510696717)
XLA Ops:
  0.6 1.0 %prep.1 = (bf16[64,1024]{1,0:T(8,128)(2,1)S(1)}, f32[64,256]{1,0:T(8,128)S(1)}, s32[2,16]{1,0:T(2,128)S(1)}) custom-call(s32[16]{0:T(128)} %pairs_hbm.1, s32[16]{0:T(128)} %slots_hbm.1, bf16[64,512]{1,0:T(8,128)(2,1)} %k_hbm.1, bf16[64,512]{1,0:T(8,128)(2,1)} %v_hbm.1), custom_call_target="tpu_custom_call" | custom-call | tf_op jit(solution)/shard_map/prep/pallas_call | solution.py:89
  1.6 3.1 %collective-permute-start.6 = (bf16[64,1024]{1,0:T(8,128)(2,1)S(1)}, bf16[64,1024]{1,0:T(8,128)(2,1)S(1)}, u32[]{:S(2)}, u32[]{:S(2)}) collective-permute-start(bf16[64,1024]{1,0:T(8,128)(2,1)S(1)} %get-tuple-element.21.refs_2_), channel_id=1, source_target_pairs={{0,4},{1,5},{2,6},{3,7},{4,0},{5,1},{6,2},{7,3},{8,12},{9,13},{10,... | collective-permute-start | bytes 393224 | tf_op jit(solution)/shard_map/ppermute | solution.py:326
  4.8 2.6 %collective-permute-start.3 = (bf16[64,1024]{1,0:T(8,128)(2,1)S(1)}, bf16[64,1024]{1,0:T(8,128)(2,1)S(1)}, u32[]{:S(2)}, u32[]{:S(2)}) collective-permute-start(bf16[64,1024]{1,0:T(8,128)(2,1)S(1)} %get-tuple-element.21.refs_2_), channel_id=1, source_target_pairs={{0,8},{1,9},{2,10},{3,11},{4,12},{5,13},{6,14},{7,15},{8,0},{9,1},... | collective-permute-start | bytes 393224 | tf_op jit(solution)/shard_map/ppermute | solution.py:326
  7.3 1.5 %collective-permute-start.9 = (bf16[64,1024]{1,0:T(8,128)(2,1)S(1)}, bf16[64,1024]{1,0:T(8,128)(2,1)S(1)}, u32[]{:S(2)}, u32[]{:S(2)}) collective-permute-start(bf16[64,1024]{1,0:T(8,128)(2,1)S(1)} %get-tuple-element.21.refs_2_), channel_id=1, source_target_pairs={{0,2},{1,3},{2,0},{3,1},{4,6},{5,7},{6,4},{7,5},{8,10},{9,11},{10,... | collective-permute-start | bytes 393224 | tf_op jit(solution)/shard_map/ppermute | solution.py:326
  8.9 0.2 collective-permute-start
  9.1 1.0 %collective-permute-done.6.refs_2_ = bf16[64,1024]{1,0:T(8,128)(2,1)S(1)} collective-permute-done((bf16[64,1024]{1,0:T(8,128)(2,1)S(1)}, bf16[64,1024]{1,0:T(8,128)(2,1)S(1)}, u32[]{:S(2)}, u32[]{:S(2)}) %collective-permute-start.6) | collective-permute-done | bytes 131104 | tf_op jit(solution)/shard_map/ppermute | solution.py:326
  10.1 1.5 %collective-permute-start.7 = (bf16[64,1024]{1,0:T(8,128)(2,1)S(1)}, bf16[64,1024]{1,0:T(8,128)(2,1)S(1)}, u32[]{:S(2)}, u32[]{:S(2)}) collective-permute-start(bf16[64,1024]{1,0:T(8,128)(2,1)S(1)} %collective-permute-done.6.refs_2_), channel_id=1, source_target_pairs={{0,2},{1,3},{2,0},{3,1},{4,6},{5,7},{6,4},{7,5},{8,10},{9,11},{10,... | collective-permute-start | bytes 393224 | tf_op jit(solution)/shard_map/ppermute | solution.py:326
  11.6 5.5 %collective-permute-done.3.refs_2_ = bf16[64,1024]{1,0:T(8,128)(2,1)S(1)} collective-permute-done((bf16[64,1024]{1,0:T(8,128)(2,1)S(1)}, bf16[64,1024]{1,0:T(8,128)(2,1)S(1)}, u32[]{:S(2)}, u32[]{:S(2)}) %collective-permute-start.3) | collective-permute-done | bytes 131104 | tf_op jit(solution)/shard_map/ppermute | solution.py:326
  17.1 2.0 %collective-permute-start.4 = (bf16[64,1024]{1,0:T(8,128)(2,1)S(1)}, bf16[64,1024]{1,0:T(8,128)(2,1)S(1)}, u32[]{:S(2)}, u32[]{:S(2)}) collective-permute-start(bf16[64,1024]{1,0:T(8,128)(2,1)S(1)} %collective-permute-done.3.refs_2_), channel_id=1, source_target_pairs={{0,2},{1,3},{2,0},{3,1},{4,6},{5,7},{6,4},{7,5},{8,10},{9,11},{10,... | collective-permute-start | bytes 393224 | tf_op jit(solution)/shard_map/ppermute | solution.py:326
  19.1 0.0 collective-permute-done.9.refs_3_
  19.2 0.1 collective-permute-start.10
  19.2 0.0 collective-permute-done.refs_2_
  19.3 0.1 collective-permute-start.1
  19.3 0.0 collective-permute-done.7.refs_3_
  19.4 0.5 %collective-permute-start.8 = (bf16[2,64,1024]{2,1,0:T(8,128)(2,1)S(1)}, bf16[2,64,1024]{2,1,0:T(8,128)(2,1)S(1)}, u32[]{:S(2)}, u32[]{:S(2)}) collective-permute-start(bf16[2,64,1024]{2,1,0:T(8,128)(2,1)S(1)} %pad_maximum_fusion.2), channel_id=1, source_target_pairs={{0,1},{1,0},{2,3},{3,2},{4,5},{5,4},{6,7},{7,6},{8,9},{9,8},{10,11... | collective-permute-start | bytes 786440 | tf_op jit(solution)/shard_map/ppermute | solution.py:326
  19.9 3.1 %collective-permute-done.4.refs_3_ = bf16[64,1024]{1,0:T(8,128)(2,1)S(1)} collective-permute-done((bf16[64,1024]{1,0:T(8,128)(2,1)S(1)}, bf16[64,1024]{1,0:T(8,128)(2,1)S(1)}, u32[]{:S(2)}, u32[]{:S(2)}) %collective-permute-start.4) | collective-permute-done | bytes 131104 | tf_op jit(solution)/shard_map/ppermute | solution.py:326
  23.0 0.1 collective-permute-start.5
  23.1 2.1 %collective-permute-done.1.refs_3_ = bf16[64,1024]{1,0:T(8,128)(2,1)S(1)} collective-permute-done((bf16[64,1024]{1,0:T(8,128)(2,1)S(1)}, bf16[64,1024]{1,0:T(8,128)(2,1)S(1)}, u32[]{:S(2)}, u32[]{:S(2)}) %collective-permute-start.1) | collective-permute-done | bytes 131104 | tf_op jit(solution)/shard_map/ppermute | solution.py:326
  25.2 0.1 collective-permute-start.2
  25.3 1.7 %turn.1.refs_1_ = bf16[2,4,128,256]{3,2,1,0:T(8,128)(2,1)S(1)} custom-call(bf16[64,4096]{1,0:T(8,128)(2,1)} %q_hbm.1, f32[64,256]{1,0:T(8,128)S(1)} %get-tuple-element.20.trig_ref), custom_call_target="tpu_custom_call" | custom-call | tf_op jit(solution)/shard_map/turn/pallas_call | solution.py:132
  26.9 0.0 collective-permute-done.10.refs_4_
  26.9 0.9 %attend.4 = (f32[8,8,256]{2,1,0:T(8,128)S(1)}, f32[8,8,256]{2,1,0:T(8,128)S(1)}, f32[2,4,128,256]{3,2,1,0:T(8,128)S(1)}, bf16[32,16,128]{2,1,0:T(8,128)(2,1)S(1)}) custom-call(s32[2,16]{1,0:T(2,128)S(1)} %get-tuple-element.19.refs_0_, bf16[2,4,128,256]{3,2,1,0:T(8,128)(2,1)S(1)} %turn.1.refs_1_, bf16[64,1024]{1,0:T(8,128)(2,1)S(1)} %get-tuple-element.21.refs_2_, ...), custom_call_target="tpu_custom_call" | custom-call | flops 201326592 | bytes 1048576 | tf_op jit(solution)/shard_map/attend/pallas_call | solution.py:311
  27.8 0.0 collective-permute-done.8.refs_4_
  27.8 1.1 %attend.5 = (f32[8,8,256]{2,1,0:T(8,128)S(1)}, f32[8,8,256]{2,1,0:T(8,128)S(1)}, f32[2,4,128,256]{3,2,1,0:T(8,128)S(1)}, bf16[32,16,128]{2,1,0:T(8,128)(2,1)S(1)}) custom-call(s32[2,16]{1,0:T(2,128)S(1)} %get-tuple-element.19.refs_0_, ...), custom_call_target="tpu_custom_call", output_to_operand_aliasing={{0}: (5, {}), {1}: (6, {}), {2}: (7, {}), {3}: (8, {})} | custom-call | flops 201326592 | bytes 1048576 | tf_op jit(solution)/shard_map/attend/pallas_call | solution.py:311
  28.9 0.0 collective-permute-done.5.refs_4_
  29.0 1.1 %attend.6 = (f32[8,8,256]{2,1,0:T(8,128)S(1)}, f32[8,8,256]{2,1,0:T(8,128)S(1)}, f32[2,4,128,256]{3,2,1,0:T(8,128)S(1)}, bf16[32,16,128]{2,1,0:T(8,128)(2,1)S(1)}) custom-call(s32[2,16]{1,0:T(2,128)S(1)} %get-tuple-element.19.refs_0_, ...), custom_call_target="tpu_custom_call", output_to_operand_aliasing={{0}: (5, {}), {1}: (6, {}), {2}: (7, {}), {3}: (8, {})} | custom-call | flops 201326592 | bytes 1048576 | tf_op jit(solution)/shard_map/attend/pallas_call | solution.py:311
  30.1 0.0 collective-permute-done.2.refs_4_
  30.1 1.7 %attend.7 = (bf16[64,4096]{1,0:T(8,128)(2,1)}, bf16[32,16,128]{2,1,0:T(8,128)(2,1)}) custom-call(s32[2,16]{1,0:T(2,128)S(1)} %get-tuple-element.19.refs_0_, bf16[2,4,128,256]{3,2,1,0:T(8,128)(2,1)S(1)} %turn.1.refs_1_, bf16[64,1024]{1,0:T(8,128)(2,1)S(1)} %collective-permute-done.refs_2_, bf16[64,1024]{1,0:T(8,128)(2,1)S(1)} %collective-permute-done.1.refs_3_, ...), custom_call_target="tpu_custom_call" | custom-call | flops 201326592 | bytes 1048576 | tf_op jit(solution)/shard_map/attend/pallas_call | solution.py:311
  (4 shorter events, 0.1 us)
Async XLA Ops:
  1.6 8.5 %collective-permute-start.6 = (bf16[64,1024]{1,0:T(8,128)(2,1)S(1)}, bf16[64,1024]{1,0:T(8,128)(2,1)S(1)}, u32[]{:S(2)}, u32[]{:S(2)}) collective-permute-start(bf16[64,1024]{1,0:T(8,128)(2,1)S(1)} %get-tuple-element.21.refs_2_), channel_id=1, source_target_pairs={{0,4},{1,5},{2,6},{3,7},{4,0},{5,1},{6,2},{7,3},{8,12},{9,13},{10,... | collective-permute-start | bytes 393224 | tf_op jit(solution)/shard_map/ppermute | solution.py:326
  4.8 12.4 %collective-permute-start.3 = (bf16[64,1024]{1,0:T(8,128)(2,1)S(1)}, bf16[64,1024]{1,0:T(8,128)(2,1)S(1)}, u32[]{:S(2)}, u32[]{:S(2)}) collective-permute-start(bf16[64,1024]{1,0:T(8,128)(2,1)S(1)} %get-tuple-element.21.refs_2_), channel_id=1, source_target_pairs={{0,8},{1,9},{2,10},{3,11},{4,12},{5,13},{6,14},{7,15},{8,0},{9,1},... | collective-permute-start | bytes 393224 | tf_op jit(solution)/shard_map/ppermute | solution.py:326
  7.3 11.8 %collective-permute-start.9 = (bf16[64,1024]{1,0:T(8,128)(2,1)S(1)}, bf16[64,1024]{1,0:T(8,128)(2,1)S(1)}, u32[]{:S(2)}, u32[]{:S(2)}) collective-permute-start(bf16[64,1024]{1,0:T(8,128)(2,1)S(1)} %get-tuple-element.21.refs_2_), channel_id=1, source_target_pairs={{0,2},{1,3},{2,0},{3,1},{4,6},{5,7},{6,4},{7,5},{8,10},{9,11},{10,... | collective-permute-start | bytes 393224 | tf_op jit(solution)/shard_map/ppermute | solution.py:326
  8.9 10.4 %collective-permute-start = (bf16[64,1024]{1,0:T(8,128)(2,1)S(1)}, bf16[64,1024]{1,0:T(8,128)(2,1)S(1)}, u32[]{:S(2)}, u32[]{:S(2)}) collective-permute-start(bf16[64,1024]{1,0:T(8,128)(2,1)S(1)} %get-tuple-element.21.refs_2_), channel_id=1, source_target_pairs={{0,12},{1,13},{2,14},{3,15},{4,8},{5,9},{6,10},{7,11},{8,4},{9,5},... | collective-permute-start | bytes 393224 | tf_op jit(solution)/shard_map/ppermute | solution.py:326
  10.1 9.2 %collective-permute-start.7 = (bf16[64,1024]{1,0:T(8,128)(2,1)S(1)}, bf16[64,1024]{1,0:T(8,128)(2,1)S(1)}, u32[]{:S(2)}, u32[]{:S(2)}) collective-permute-start(bf16[64,1024]{1,0:T(8,128)(2,1)S(1)} %collective-permute-done.6.refs_2_), channel_id=1, source_target_pairs={{0,2},{1,3},{2,0},{3,1},{4,6},{5,7},{6,4},{7,5},{8,10},{9,11},{10,... | collective-permute-start | bytes 393224 | tf_op jit(solution)/shard_map/ppermute | solution.py:326
  17.1 5.9 %collective-permute-start.4 = (bf16[64,1024]{1,0:T(8,128)(2,1)S(1)}, bf16[64,1024]{1,0:T(8,128)(2,1)S(1)}, u32[]{:S(2)}, u32[]{:S(2)}) collective-permute-start(bf16[64,1024]{1,0:T(8,128)(2,1)S(1)} %collective-permute-done.3.refs_2_), channel_id=1, source_target_pairs={{0,2},{1,3},{2,0},{3,1},{4,6},{5,7},{6,4},{7,5},{8,10},{9,11},{10,... | collective-permute-start | bytes 393224 | tf_op jit(solution)/shard_map/ppermute | solution.py:326
  19.2 7.8 %collective-permute-start.10 = (bf16[2,64,1024]{2,1,0:T(8,128)(2,1)S(1)}, bf16[2,64,1024]{2,1,0:T(8,128)(2,1)S(1)}, u32[]{:S(2)}, u32[]{:S(2)}) collective-permute-start(bf16[2,64,1024]{2,1,0:T(8,128)(2,1)S(1)} %pad_maximum_fusion.3), channel_id=1, source_target_pairs={{0,1},{1,0},{2,3},{3,2},{4,5},{5,4},{6,7},{7,6},{8,9},{9,8},{10,11... | collective-permute-start | bytes 786440 | tf_op jit(solution)/shard_map/ppermute | solution.py:326
  19.3 5.9 %collective-permute-start.1 = (bf16[64,1024]{1,0:T(8,128)(2,1)S(1)}, bf16[64,1024]{1,0:T(8,128)(2,1)S(1)}, u32[]{:S(2)}, u32[]{:S(2)}) collective-permute-start(bf16[64,1024]{1,0:T(8,128)(2,1)S(1)} %collective-permute-done.refs_2_), channel_id=1, source_target_pairs={{0,2},{1,3},{2,0},{3,1},{4,6},{5,7},{6,4},{7,5},{8,10},{9,11},{10,... | collective-permute-start | bytes 393224 | tf_op jit(solution)/shard_map/ppermute | solution.py:326
  19.4 8.5 %collective-permute-start.8 = (bf16[2,64,1024]{2,1,0:T(8,128)(2,1)S(1)}, bf16[2,64,1024]{2,1,0:T(8,128)(2,1)S(1)}, u32[]{:S(2)}, u32[]{:S(2)}) collective-permute-start(bf16[2,64,1024]{2,1,0:T(8,128)(2,1)S(1)} %pad_maximum_fusion.2), channel_id=1, source_target_pairs={{0,1},{1,0},{2,3},{3,2},{4,5},{5,4},{6,7},{7,6},{8,9},{9,8},{10,11... | collective-permute-start | bytes 786440 | tf_op jit(solution)/shard_map/ppermute | solution.py:326
  23.0 6.0 %collective-permute-start.5 = (bf16[2,64,1024]{2,1,0:T(8,128)(2,1)S(1)}, bf16[2,64,1024]{2,1,0:T(8,128)(2,1)S(1)}, u32[]{:S(2)}, u32[]{:S(2)}) collective-permute-start(bf16[2,64,1024]{2,1,0:T(8,128)(2,1)S(1)} %pad_maximum_fusion.1), channel_id=1, source_target_pairs={{0,1},{1,0},{2,3},{3,2},{4,5},{5,4},{6,7},{7,6},{8,9},{9,8},{10,11... | collective-permute-start | bytes 786440 | tf_op jit(solution)/shard_map/ppermute | solution.py:326
  25.2 4.9 %collective-permute-start.2 = (bf16[2,64,1024]{2,1,0:T(8,128)(2,1)S(1)}, bf16[2,64,1024]{2,1,0:T(8,128)(2,1)S(1)}, u32[]{:S(2)}, u32[]{:S(2)}) collective-permute-start(bf16[2,64,1024]{2,1,0:T(8,128)(2,1)S(1)} %pad_maximum_fusion), channel_id=1, source_target_pairs={{0,1},{1,0},{2,3},{3,2},{4,5},{5,4},{6,7},{7,6},{8,9},{9,8},{10,11... | collective-permute-start | bytes 786440 | tf_op jit(solution)/shard_map/ppermute | solution.py:326
